TPU v7x, 32 devices: a whole 2x2x4 slice. The times are simulated.
32 devices in a mesh: lat: 8 (over y, x, core), rad: 4 (over z).
Axes of the slice: x: 2, y: 2, z: 4, core: 2. Of those that a mesh axis runs over, the one named last changes fastest.
Arguments:
- schur_off: bfloat16 [8, 4, 1536, 1536], P('lat', 'rad'), may hold values from -0.15625 to 0.15625
- schur_diag: float32 [8, 4, 1536], P('lat', 'rad'), may hold values from 1.5 to 4
- source: float32 [8, 4, 1536, 128], P('lat', 'rad'), may hold values from -6 to 6
- start: float32 [8, 4, 1536, 128], P('lat', 'rad'), may hold values from -6 to 6
- decay: float32 [8, 4, 256, 128], P('lat', 'rad'), may hold values from 0.2 to 1
- neighbour_face: int32 [8, 4], replicated, may hold values from 0 to 3
- orientation: int32 [8, 4], replicated, may hold values from 0 to 7
Outputs:
- traces: float32 [8, 4, 1536, 128], P('lat', 'rad')
Inputs may be any that keep to these rules, and one draw needn't show every extreme that they name: `neighbour_face`: a face index of 0 to 3. `orientation`: a code of 0 to 7 whose bits select transpose, row reflection and column reflection.
All inputs are finite; a program needn't handle non-finite values.
Results may differ from a plain program's by a relative error of at most 0.001.
Values sent between devices are 32-bit elements; how exact they have to be, the bound alone decides.
A program may use at most 64 MiB of HBM per device.

v0:
```python
import jax
import jax.numpy as jnp
from jax import lax
from jax.sharding import PartitionSpec as P

FACE_SIDE = 16
ITERS = 2
RADIAL_PASSES = 2


OMEGA = 0.3
COUPLE = 0.5


def from_behind(value, axis, steps):
    count = lax.axis_size(axis)
    pairs = [(source, (source + steps) % count) for source in range(count)]
    return lax.ppermute(value, axis, pairs)


def prefix(shard, axis, combine, identity):
    count, index = (lax.axis_size(axis), lax.axis_index(axis))
    everything = jax.tree.map(lambda part: lax.all_gather(part, axis), shard)
    start = jax.tree.map(
        lambda part, zero: jnp.broadcast_to(jnp.asarray(zero, part.dtype), part.shape),
        shard,
        identity,
    )

    def lap(k, before):
        reached = k < index
        new = combine(before, jax.tree.map(lambda part: part[k], everything))
        return jax.tree.map(lambda a, b: jnp.where(reached, a, b), new, before)

    return lax.fori_loop(0, count, lap, start)


def shifted(block, axis, distance):
    devices = range(lax.axis_size(axis))
    route = [(i - distance, i) for i in devices if i - distance in devices]
    return lax.ppermute(block, axis, route)


def apply_block(weight, diag, trace):
    return (
        jnp.dot(weight, trace.astype(jnp.bfloat16), preferred_element_type=jnp.float32)
        + diag[:, None] * trace
    )


def select_face(lateral, which):
    codes = jnp.arange(4, dtype=jnp.int32)
    weights = (codes == which).astype(jnp.float32)
    return jnp.sum(lateral * weights[:, None, None], axis=0)


def orient_face(face, code):
    side = FACE_SIDE
    grid = face.reshape(side, side, face.shape[1])
    grid = jnp.where(code & 2 != 0, grid[::-1], grid)
    grid = jnp.where(code & 4 != 0, grid[:, ::-1], grid)
    grid = jnp.where(code & 1 != 0, jnp.transpose(grid, (1, 0, 2)), grid)
    return grid.reshape(side * side, face.shape[1])


def link_compose(earlier, later):
    return (earlier[0] * later[0], earlier[1] * later[0] + later[1])


def per_device(schur_off, schur_diag, source, start, decay, neighbour_face, orientation):
    weight = schur_off[0, 0]
    diag = schur_diag[0, 0]
    rhs = source[0, 0]
    trace = start[0, 0]
    factor = decay[0, 0]
    nodes = trace.shape[0] // 6
    columns = trace.shape[1]
    lat_count = lax.axis_size("lat")
    far = max(2, lat_count // 8)
    offsets = (-1, 1, -far, far)
    patch = lax.axis_index("lat")
    blank = jnp.zeros((nodes, columns), jnp.float32)
    for outer in range(ITERS):
        applied = apply_block(weight, diag, trace)
        lateral = trace[: 4 * nodes].reshape(4, nodes, columns)
        incoming = []
        for k in range(4):
            target = (patch - offsets[k]) % lat_count
            face = select_face(lateral, neighbour_face[target, k])
            ready = orient_face(face, orientation[target, k])
            incoming.append(from_behind(ready, "lat", -offsets[k]))
        coupling = jnp.concatenate(incoming + [blank, blank], axis=0)
        trace = trace + OMEGA * (rhs - applied + COUPLE * coupling)
        for sweep in range(RADIAL_PASSES):
            res = rhs - apply_block(weight, diag, trace)
            bottom = res[4 * nodes : 5 * nodes]
            top = res[5 * nodes :]
            unused, inflow = prefix(
                (factor, factor * top), "rad", link_compose, (jnp.ones_like(factor), blank)
            )
            above = shifted(bottom, "rad", -1)
            coupling = jnp.concatenate(
                [jnp.zeros((4 * nodes, columns), jnp.float32), inflow, above], axis=0
            )
            trace = trace + OMEGA * (res + COUPLE * coupling)
    return trace[None, None]


def solution(mesh):
    return jax.shard_map(
        per_device,
        mesh=mesh,
        in_specs=(
            P("lat", "rad", None, None),
            P("lat", "rad", None),
            P("lat", "rad", None, None),
            P("lat", "rad", None, None),
            P("lat", "rad", None, None),
            P(),
            P(),
        ),
        out_specs=P("lat", "rad", None, None),
        check_vma=False,
    )
```

profile of v0, /device:TPU:0, one launch (start us, length us, event | category | flops | bytes accessed | tf_op | source)
XLA Modules:
  0.0 175.8 jit_solution(2327398596433622296)
XLA Ops:
  0.0 1.6 constant_dynamic-slice_fusion.1
  1.6 0.6 compare_convert_fusion
  2.2 0.6 compare_convert_fusion.1
  2.8 0.7 compare_convert_fusion.2
  3.5 0.7 compare_convert_fusion.3
  4.2 1.1 slice.31
  6.0 0.2 multiply_reduce_fusion.4
  7.6 0.7 copy_select_fusion
  8.3 4.0 %collective-permute-start.3 = (f32[256,128]{1,0:T(8,128)}, f32[256,128]{1,0:T(8,128)}, u32[]{:S(2)}, u32[]{:S(2)}) collective-permute-start(f32[256,128]{1,0:T(8,128)} %bitcast.32), channel_id=1, source_target_pairs={{0,24},{4,28},{8,0},{12,4},{16,8},{20,12},{24,16},{28,20},{1,25},{... | collective-permute-start | bytes 393224 | tf_op jit(solution)/shard_map/ppermute | solution.py:18
  14.5 0.7 copy_select_fusion.1
  17.2 0.7 copy_select_fusion.2
  17.9 1.8 %collective-permute-start.1 = (f32[256,128]{1,0:T(8,128)}, f32[256,128]{1,0:T(8,128)}, u32[]{:S(2)}, u32[]{:S(2)}) collective-permute-start(f32[256,128]{1,0:T(8,128)} %bitcast.18), channel_id=1, source_target_pairs={{0,28},{4,0},{8,4},{12,8},{16,12},{20,16},{24,20},{28,24},{1,29},{... | collective-permute-start | bytes 393224 | tf_op jit(solution)/shard_map/ppermute | solution.py:18
  21.6 0.7 copy_select_fusion.3
  22.4 3.8 %fusion.19 = f32[1536,128]{1,0:T(8,128)S(1)} fusion(bf16[1,1,1536,1536]{3,2,1,0:T(8,128)(2,1)} %param.15, f32[1,1,1536,128]{3,2,1,0:T(8,128)S(1)} %copy-done, f32[1,1,1536,128]{3,2,1,0:T(8,128)S(1)} %copy-done.1, f32[1536]{0:T(1024)S(1)} %reduce), kind=kOutput, calls=%fused_computation.25 | convolution fusion | flops 604766208 | bytes 7084032 | tf_op jit(solution)/shard_map/dot_general | solution.py:46
  26.1 16.3 %all-gather = f32[4,1,256,128]{3,2,1,0:T(8,128)S(1)} all-gather(f32[1,1,256,128]{3,2,1,0:T(8,128)S(1)} %copy-done.5), channel_id=2, replica_groups=mesh['lat'=8,'rad'=4] {'rad'}, dimensions={0}, use_global_device_ids=true | all-gather | bytes 655360 | tf_op jit(solution)/shard_map/all_gather | solution.py:23
  42.5 0.9 constant_dynamic-update-slice_fusion.3
  43.4 0.9 constant_dynamic-update-slice_fusion.2
  44.3 0.9 constant_dynamic-update-slice_fusion.1
  45.3 0.9 constant_dynamic-update-slice_fusion
  46.2 4.1 %fusion.64 = f32[1536,128]{1,0:T(8,128)S(1)} fusion(bf16[1,1,1536,1536]{3,2,1,0:T(8,128)(2,1)} %param.15, f32[1,1,1536,128]{3,2,1,0:T(8,128)S(1)} %copy-done, f32[1536,128]{1,0:T(8,128)S(1)} %fusion.19, f32[1536,128]{1,0:T(8,128)S(1)} %broadcast_dynamic-update-slice_fusion.1, f32[1,1,1536,128]{3,2,1,0:T(8,128)S(1)} %copy-done.1, f32[1536]{0:T(1024)S(1)} %reduce), kind=kOutput, calls=%fused_computation.40 | convolution fusion | flops 606339072 | bytes 8656896 | tf_op jit(solution)/shard_map/dot_general | solution.py:46
  50.4 0.9 copy-done.3
  51.3 0.7 slice_multiply_fusion.3
  51.9 16.2 %all-gather.1 = f32[1024,128]{1,0:T(8,128)} all-gather(f32[256,128]{1,0:T(8,128)S(1)} %get-tuple-element.511), channel_id=3, replica_groups=mesh['lat'=8,'rad'=4] {'rad'}, dimensions={0}, use_global_device_ids=true | all-gather | bytes 655360 | tf_op jit(solution)/shard_map/all_gather | solution.py:23
  68.2 1.3 collective-permute-start.4
  69.5 4.1 %while.56 = (s32[]{:T(128)}, f32[256,128]{1,0:T(8,128)S(1)}, s32[]{:T(128)}, f32[4,256,128]{2,1,0:T(8,128)S(1)}, f32[4,256,128]{2,1,0:T(8,128)}, /*index=5*/s32[]{:T(128)}, s32[]{:T(128)}) while((s32[]{:T(128)}, f32[256,128]{1,0:T(8,128)S(1)}, s32[]{:T(128)}, f32[4,256,128]{2,1,0:T(8,128)S(1)}, f32[4,256,128]{2,1,0:T(8,128)}, ...), condition=%wide.region_5.6_spmd.clone, body=%wide.region_4.5_spmd.clone.sunk | while | flops 131076 | bytes 524389 | solution.py:35
  69.5 1.0 fusion.110
  70.5 1.0 fusion.110
  71.5 1.0 fusion.110
  72.6 1.0 fusion.110
  73.6 1.8 %collective-permute-done.4 = f32[256,128]{1,0:T(8,128)} collective-permute-done((f32[256,128]{1,0:T(8,128)}, f32[256,128]{1,0:T(8,128)}, u32[]{:S(2)}, u32[]{:S(2)}) %collective-permute-start.4) | collective-permute-done | bytes 131104 | tf_op jit(solution)/shard_map/ppermute | solution.py:41
  75.3 1.7 fusion.69
  77.0 4.0 %fusion.55 = f32[1536,128]{1,0:T(8,128)S(1)} fusion(bf16[1,1,1536,1536]{3,2,1,0:T(8,128)(2,1)} %param.15, f32[1,1,1536,128]{3,2,1,0:T(8,128)S(1)} %copy-done, f32[1536,128]{1,0:T(8,128)S(1)} %fusion.69, f32[1536]{0:T(1024)S(1)} %reduce), kind=kOutput, calls=%fused_computation.37 | convolution fusion | flops 604766208 | bytes 7084032 | tf_op jit(solution)/shard_map/dot_general | solution.py:46
  81.1 16.0 %all-gather.2 = f32[1024,128]{1,0:T(8,128)S(1)} all-gather(f32[256,128]{1,0:T(8,128)S(1)} %get-tuple-element.509), channel_id=4, replica_groups=mesh['lat'=8,'rad'=4] {'rad'}, dimensions={0}, use_global_device_ids=true | all-gather | bytes 655360 | tf_op jit(solution)/shard_map/all_gather | solution.py:23
  97.1 1.3 collective-permute-start.5
  98.4 0.3 while.57
  98.4 0.1 fusion.111
  98.6 0.1 fusion.111
  98.8 5.2 %collective-permute-done.5 = f32[256,128]{1,0:T(8,128)S(1)} collective-permute-done((f32[256,128]{1,0:T(8,128)S(1)}, f32[256,128]{1,0:T(8,128)S(1)}, u32[]{:S(2)}, u32[]{:S(2)}) %collective-permute-start.5) | collective-permute-done | bytes 131104 | tf_op jit(solution)/shard_map/ppermute | solution.py:41
  104.0 1.4 fusion.72
  105.4 1.0 multiply_reduce_fusion
  106.5 1.9 %collective-permute-start.9 = (f32[256,128]{1,0:T(8,128)S(1)}, f32[256,128]{1,0:T(8,128)S(1)}, u32[]{:S(2)}, u32[]{:S(2)}) collective-permute-start(f32[256,128]{1,0:T(8,128)S(1)} %bitcast.256), channel_id=1, source_target_pairs={{0,24},{4,28},{8,0},{12,4},{16,8},{20,12},{24,16},{28,20},{1,25},{... | collective-permute-start | bytes 393224 | tf_op jit(solution)/shard_map/ppermute | solution.py:18
  108.8 0.5 collective-permute-start.6
  109.4 0.2 collective-permute-start.8
  109.6 5.8 %collective-permute-done.6 = f32[256,128]{1,0:T(8,128)S(1)} collective-permute-done((f32[256,128]{1,0:T(8,128)S(1)}, f32[256,128]{1,0:T(8,128)S(1)}, u32[]{:S(2)}, u32[]{:S(2)}) %collective-permute-start.6) | collective-permute-done | bytes 131104 | tf_op jit(solution)/shard_map/ppermute | solution.py:18
  115.5 1.2 collective-permute-done.8
  116.8 3.9 %fusion.86 = f32[1536,128]{1,0:T(8,128)S(1)} fusion(f32[1536,128]{1,0:T(8,128)S(1)} %fusion.72, bf16[1,1,1536,1536]{3,2,1,0:T(8,128)(2,1)} %param.15, f32[1,1,1536,128]{3,2,1,0:T(8,128)S(1)} %copy-done, f32[1536,128]{1,0:T(8,128)S(1)} %broadcast_dynamic-update-slice_fusion, f32[1536]{0:T(1024)S(1)} %reduce), kind=kOutput, calls=%fused_computation.60 | convolution fusion | flops 605552640 | bytes 7870464 | tf_op jit(solution)/shard_map/dot_general | solution.py:46
  120.7 1.4 fusion.37
  122.2 16.9 %all-gather.3 = f32[1024,128]{1,0:T(8,128)} all-gather(f32[256,128]{1,0:T(8,128)S(1)} %get-tuple-element.507), channel_id=5, replica_groups=mesh['lat'=8,'rad'=4] {'rad'}, dimensions={0}, use_global_device_ids=true | all-gather | bytes 655360 | tf_op jit(solution)/shard_map/all_gather | solution.py:23
  139.1 1.3 collective-permute-start.10
  140.4 4.1 %while.58 = (s32[]{:T(128)}, f32[256,128]{1,0:T(8,128)S(1)}, s32[]{:T(128)}, f32[4,256,128]{2,1,0:T(8,128)S(1)}, f32[4,256,128]{2,1,0:T(8,128)}, /*index=5*/s32[]{:T(128)}, s32[]{:T(128)}) while((s32[]{:T(128)}, f32[256,128]{1,0:T(8,128)S(1)}, s32[]{:T(128)}, f32[4,256,128]{2,1,0:T(8,128)S(1)}, f32[4,256,128]{2,1,0:T(8,128)}, ...), condition=%wide.region_13.14_spmd.clone, body=%wide.region_12.13_spmd.clone.sunk | while | flops 131076 | bytes 524389 | solution.py:35
  140.4 1.0 fusion.112
  141.4 1.0 fusion.112
  142.4 1.0 fusion.112
  143.5 1.0 fusion.112
  144.5 1.4 collective-permute-done.10
  145.9 3.8 %fusion.28 = f32[1536,128]{1,0:T(8,128)S(1)} fusion(bf16[1,1,1536,1536]{3,2,1,0:T(8,128)(2,1)} %param.15, f32[1,1,1536,128]{3,2,1,0:T(8,128)S(1)} %copy-done, f32[1536]{0:T(1024)S(1)} %reduce, f32[1536,128]{1,0:T(8,128)S(1)} %fusion.86, f32[1536,128]{1,0:T(8,128)S(1)} %fusion.37, f32[256,128]{1,0:T(8,128)S(1)} %collective-permute-done.10, ...), kind=kOutput, calls=%fused_computation.28 | convolution fusion | flops 607125504 | bytes 8138752 | tf_op jit(solution)/shard_map/dot_general | solution.py:46
  149.8 0.8 copy-done.6
  150.7 16.0 %all-gather.4 = f32[1024,128]{1,0:T(8,128)S(1)} all-gather(f32[256,128]{1,0:T(8,128)S(1)} %get-tuple-element.505), channel_id=6, replica_groups=mesh['lat'=8,'rad'=4] {'rad'}, dimensions={0}, use_global_device_ids=true | all-gather | bytes 655360 | tf_op jit(solution)/shard_map/all_gather | solution.py:23
  166.7 1.3 collective-permute-start.11
  168.0 0.3 while.59
  168.0 0.1 fusion.113
  168.2 0.1 fusion.113
  168.3 5.2 %collective-permute-done.11 = f32[256,128]{1,0:T(8,128)S(1)} collective-permute-done((f32[256,128]{1,0:T(8,128)S(1)}, f32[256,128]{1,0:T(8,128)S(1)}, u32[]{:S(2)}, u32[]{:S(2)}) %collective-permute-start.11) | collective-permute-done | bytes 131104 | tf_op jit(solution)/shard_map/ppermute | solution.py:41
  173.5 2.3 %fusion.79 = f32[1,1,1536,128]{3,2,1,0:T(8,128)} fusion(f32[1536,128]{1,0:T(8,128)} %copy-done.6, f32[256,128]{1,0:T(8,128)S(1)} %collective-permute-done.11, f32[256,128]{1,0:T(8,128)S(1)} %get-tuple-element.384, f32[1536]{0:T(1024)S(1)} %pad.9.clone, f32[1536,128]{1,0:T(8,128)S(1)} %fusion.86, f32[1536,128]{1,0:T(8,128)S(1)} %fusion.37, ...), kind=kLoop, calls=%fused_computation.57 | loop fusion | flops 2359296 | bytes 3676160 | tf_op jit(solution)/shard_map/broadcast_in_dim | solution.py:106
  (85 shorter events, 1.2 us)
Async XLA Ops:
  0.0 22.3 %copy-start.1 = (f32[1,1,1536,128]{3,2,1,0:T(8,128)S(1)}, f32[1,1,1536,128]{3,2,1,0:T(8,128)}, u32[]{:S(2)}) copy-start(f32[1,1,1536,128]{3,2,1,0:T(8,128)} %param.18) | copy-start | bytes 2359300
  0.0 22.3 %copy-start.7 = (f32[1,1,1536]{2,1,0:T(1,128)S(1)}, f32[1,1,1536]{2,1,0:T(1,128)}, u32[]{:S(2)}) copy-start(f32[1,1,1536]{2,1,0:T(1,128)} %param.16) | copy-start | bytes 18436
  0.0 22.3 %copy-start = (f32[1,1,1536,128]{3,2,1,0:T(8,128)S(1)}, f32[1,1,1536,128]{3,2,1,0:T(8,128)}, u32[]{:S(2)}) copy-start(f32[1,1,1536,128]{3,2,1,0:T(8,128)} %param.17) | copy-start | bytes 2359300
  2.2 4.0 %copy-start.8 = (f32[4]{0:T(128)}, f32[4]{0:T(128)S(1)}, u32[]{:S(2)}) copy-start(f32[4]{0:T(128)S(1)} %compare_convert_fusion) | copy-start | bytes 52
  2.8 3.4 %copy-start.9 = (f32[4]{0:T(128)}, f32[4]{0:T(128)S(1)}, u32[]{:S(2)}) copy-start(f32[4]{0:T(128)S(1)} %compare_convert_fusion.1) | copy-start | bytes 52
  3.5 2.7 %copy-start.10 = (f32[4]{0:T(128)}, f32[4]{0:T(128)S(1)}, u32[]{:S(2)}) copy-start(f32[4]{0:T(128)S(1)} %compare_convert_fusion.2) | copy-start | bytes 52
  4.2 2.0 %copy-start.11 = (f32[4]{0:T(128)}, f32[4]{0:T(128)S(1)}, u32[]{:S(2)}) copy-start(f32[4]{0:T(128)S(1)} %compare_convert_fusion.3) | copy-start | bytes 52
  8.3 36.9 %collective-permute-start.3 = (f32[256,128]{1,0:T(8,128)}, f32[256,128]{1,0:T(8,128)}, u32[]{:S(2)}, u32[]{:S(2)}) collective-permute-start(f32[256,128]{1,0:T(8,128)} %bitcast.32), channel_id=1, source_target_pairs={{0,24},{4,28},{8,0},{12,4},{16,8},{20,12},{24,16},{28,20},{1,25},{... | collective-permute-start | bytes 393224 | tf_op jit(solution)/shard_map/ppermute | solution.py:18
  15.2 29.1 %collective-permute-start.2 = (f32[256,128]{1,0:T(8,128)}, f32[256,128]{1,0:T(8,128)}, u32[]{:S(2)}, u32[]{:S(2)}) collective-permute-start(f32[256,128]{1,0:T(8,128)} %bitcast.25), channel_id=1, source_target_pairs={{0,8},{4,12},{8,16},{12,20},{16,24},{20,28},{24,0},{28,4},{1,9},{5... | collective-permute-start | bytes 393224 | tf_op jit(solution)/shard_map/ppermute | solution.py:18
  17.9 25.5 %collective-permute-start.1 = (f32[256,128]{1,0:T(8,128)}, f32[256,128]{1,0:T(8,128)}, u32[]{:S(2)}, u32[]{:S(2)}) collective-permute-start(f32[256,128]{1,0:T(8,128)} %bitcast.18), channel_id=1, source_target_pairs={{0,28},{4,0},{8,4},{12,8},{16,12},{20,16},{24,20},{28,24},{1,29},{... | collective-permute-start | bytes 393224 | tf_op jit(solution)/shard_map/ppermute | solution.py:18
  22.3 3.8 %copy-start.5 = (f32[1,1,256,128]{3,2,1,0:T(8,128)S(1)}, f32[1,1,256,128]{3,2,1,0:T(8,128)}, u32[]{:S(2)}) copy-start(f32[1,1,256,128]{3,2,1,0:T(8,128)} %param.19) | copy-start | bytes 393220
  22.3 20.2 %collective-permute-start = (f32[256,128]{1,0:T(8,128)}, f32[256,128]{1,0:T(8,128)}, u32[]{:S(2)}, u32[]{:S(2)}) collective-permute-start(f32[256,128]{1,0:T(8,128)} %bitcast.11), channel_id=1, source_target_pairs={{0,4},{4,8},{8,12},{12,16},{16,20},{20,24},{24,28},{28,0},{1,5},{5... | collective-permute-start | bytes 393224 | tf_op jit(solution)/shard_map/ppermute | solution.py:18
  46.2 4.2 %copy-start.4 = (f32[1536,128]{1,0:T(8,128)}, f32[1536,128]{1,0:T(8,128)S(1)}, u32[]{:S(2)}) copy-start(f32[1536,128]{1,0:T(8,128)S(1)} %broadcast_dynamic-update-slice_fusion.1) | copy-start | bytes 2359300
  50.4 0.9 copy-start.3
  68.2 7.2 %collective-permute-start.4 = (f32[256,128]{1,0:T(8,128)}, f32[256,128]{1,0:T(8,128)}, u32[]{:S(2)}, u32[]{:S(2)}) collective-permute-start(f32[256,128]{1,0:T(8,128)} %get-tuple-element.512), channel_id=1, source_target_pairs={{1,0},{2,1},{3,2},{5,4},{6,5},{7,6},{9,8},{10,9},{11,10},{13,12},{... | collective-permute-start | bytes 393224 | tf_op jit(solution)/shard_map/ppermute | solution.py:41
  77.0 4.1 %copy-start.2 = (f32[1536,128]{1,0:T(8,128)}, f32[1536,128]{1,0:T(8,128)S(1)}, u32[]{:S(2)}) copy-start(f32[1536,128]{1,0:T(8,128)S(1)} %fusion.69) | copy-start | bytes 2359300
  97.1 6.9 %collective-permute-start.5 = (f32[256,128]{1,0:T(8,128)S(1)}, f32[256,128]{1,0:T(8,128)S(1)}, u32[]{:S(2)}, u32[]{:S(2)}) collective-permute-start(f32[256,128]{1,0:T(8,128)S(1)} %get-tuple-element.510), channel_id=1, source_target_pairs={{1,0},{2,1},{3,2},{5,4},{6,5},{7,6},{9,8},{10,9},{11,10},{13,12},{... | collective-permute-start | bytes 393224 | tf_op jit(solution)/shard_map/ppermute | solution.py:41
  106.5 10.2 %collective-permute-start.9 = (f32[256,128]{1,0:T(8,128)S(1)}, f32[256,128]{1,0:T(8,128)S(1)}, u32[]{:S(2)}, u32[]{:S(2)}) collective-permute-start(f32[256,128]{1,0:T(8,128)S(1)} %bitcast.256), channel_id=1, source_target_pairs={{0,24},{4,28},{8,0},{12,4},{16,8},{20,12},{24,16},{28,20},{1,25},{... | collective-permute-start | bytes 393224 | tf_op jit(solution)/shard_map/ppermute | solution.py:18
  108.6 6.9 %collective-permute-start.7 = (f32[256,128]{1,0:T(8,128)S(1)}, f32[256,128]{1,0:T(8,128)S(1)}, u32[]{:S(2)}, u32[]{:S(2)}) collective-permute-start(f32[256,128]{1,0:T(8,128)S(1)} %bitcast.257), channel_id=1, source_target_pairs={{0,28},{4,0},{8,4},{12,8},{16,12},{20,16},{24,20},{28,24},{1,29},{... | collective-permute-start | bytes 393224 | tf_op jit(solution)/shard_map/ppermute | solution.py:18
  108.8 6.6 %collective-permute-start.6 = (f32[256,128]{1,0:T(8,128)S(1)}, f32[256,128]{1,0:T(8,128)S(1)}, u32[]{:S(2)}, u32[]{:S(2)}) collective-permute-start(f32[256,128]{1,0:T(8,128)S(1)} %bitcast.259), channel_id=1, source_target_pairs={{0,4},{4,8},{8,12},{12,16},{16,20},{20,24},{24,28},{28,0},{1,5},{5... | collective-permute-start | bytes 393224 | tf_op jit(solution)/shard_map/ppermute | solution.py:18
  109.4 7.3 %collective-permute-start.8 = (f32[256,128]{1,0:T(8,128)S(1)}, f32[256,128]{1,0:T(8,128)S(1)}, u32[]{:S(2)}, u32[]{:S(2)}) collective-permute-start(f32[256,128]{1,0:T(8,128)S(1)} %bitcast.258), channel_id=1, source_target_pairs={{0,8},{4,12},{8,16},{12,20},{16,24},{20,28},{24,0},{28,4},{1,9},{5... | collective-permute-start | bytes 393224 | tf_op jit(solution)/shard_map/ppermute | solution.py:18
  116.7 4.0 %slice-start = ((s8[4718592]{0:T(1024)(128)(4,1)}), s8[4194304]{0:T(1024)(128)(4,1)S(1)}, s32[]{:S(2)}) async-start(s8[4718592]{0:T(1024)(128)(4,1)} %bitcast.227), calls=%async_computation | async-start | bytes 8388608
  116.8 3.9 %slice-start.1 = ((s8[4718592]{0:T(1024)(128)(4,1)}), s8[524288]{0:T(1024)(128)(4,1)S(1)}, s32[]{:S(2)}) async-start(s8[4718592]{0:T(1024)(128)(4,1)} %bitcast.227), calls=%async_computation.1 | async-start | bytes 1048576
  139.1 6.9 %collective-permute-start.10 = (f32[256,128]{1,0:T(8,128)S(1)}, f32[256,128]{1,0:T(8,128)S(1)}, u32[]{:S(2)}, u32[]{:S(2)}) collective-permute-start(f32[256,128]{1,0:T(8,128)S(1)} %get-tuple-element.508), channel_id=1, source_target_pairs={{1,0},{2,1},{3,2},{5,4},{6,5},{7,6},{9,8},{10,9},{11,10},{13,12},{... | collective-permute-start | bytes 393224 | tf_op jit(solution)/shard_map/ppermute | solution.py:41
  149.8 0.9 copy-start.6
  166.7 6.9 %collective-permute-start.11 = (f32[256,128]{1,0:T(8,128)S(1)}, f32[256,128]{1,0:T(8,128)S(1)}, u32[]{:S(2)}, u32[]{:S(2)}) collective-permute-start(f32[256,128]{1,0:T(8,128)S(1)} %get-tuple-element.506), channel_id=1, source_target_pairs={{1,0},{2,1},{3,2},{5,4},{6,5},{7,6},{9,8},{10,9},{11,10},{13,12},{... | collective-permute-start | bytes 393224 | tf_op jit(solution)/shard_map/ppermute | solution.py:41
where the time goes:
time: 177 us; the launch traced here: 176 us
  blocking collectives  81.5 us (46%)
  other arithmetic  21.8 us (12%)
  matrix products  21.1 us (12%)
  waiting for transfers between devices  20.7 us (12%)
  starting transfers between devices  13.7 us (8%)
  between operations  8.44 us (5%)
  local copies, waits for them, and re-layouts  8.36 us (5%)
    all_gather x5, blocking collectives, prefix(): everything = jax.tree.map(lambda part: lax.all_gather(part, axis), shard)  81.5 us
    dot_general x6, matrix products, apply_block(): jnp.dot(weight, trace.astype(jnp.bfloat16), preferred_element_type=jnp.fl...  21.1 us
    ppermute x4, waiting for transfers between devices, shifted(): return lax.ppermute(block, axis, route)  13.6 us
    select_n x16, other arithmetic, lap(): return jax.tree.map(lambda a, b: jnp.where(reached, a, b), new, before)  8.56 us
    ppermute x8, starting transfers between devices, from_behind(): return lax.ppermute(value, axis, pairs)  8.55 us
    ppermute x8, waiting for transfers between devices, from_behind(): return lax.ppermute(value, axis, pairs)  7.06 us
    unnamed x36, local copies, waits for them, and re-layouts  5.47 us
    ppermute x4, starting transfers between devices, shifted(): return lax.ppermute(block, axis, route)  5.13 us
  transfers between devices with their start and end apart: 12, of which 6 were waited for; matrix products, arithmetic and copies ran while one was open for 10% of the time, Pallas kernels for 0%

commit v1 on v0

v1 whole, which is shorter than its diff:
```python
import functools
import math

import jax
import jax.numpy as jnp
from jax import lax
from jax.experimental import pallas as pl
from jax.experimental.pallas import tpu as pltpu
from jax.sharding import PartitionSpec as P

ITERS = 2
RADIAL_PASSES = 2
OMEGA = 0.3
COUPLE = 0.5
CHUNKS = 4
SEND_ORDER = (2, 3, 0, 1)
MESH = pl.DeviceIdType.MESH


def permuted(face, code, side):
    nodes = side * side
    n = lax.broadcasted_iota(jnp.int32, (nodes, 1), 0)
    i, j = n // side, n % side
    swap, rows, cols = code & 1, (code >> 1) & 1, (code >> 2) & 1
    a = i + swap * (j - i)
    b = j + swap * (i - j)
    a = a + rows * (side - 1 - 2 * a)
    b = b + cols * (side - 1 - 2 * b)
    at = lax.broadcasted_iota(jnp.int32, (nodes, nodes), 1)
    hot = jnp.where(at == a * side + b, 1.0, 0.0).astype(jnp.bfloat16)
    high = face.astype(jnp.bfloat16)
    rest = face - high.astype(jnp.float32)
    middle = rest.astype(jnp.bfloat16)
    low = (rest - middle.astype(jnp.float32)).astype(jnp.bfloat16)
    total = None
    for part in (low, middle, high):
        moved = jnp.dot(hot, part, preferred_element_type=jnp.float32)
        total = moved if total is None else total + moved
    return total


def kernel(
    lat_count, rad_count, nodes,
    face_at, code_at, diag_ref, w_hbm, source_hbm, start_hbm, decay_hbm,
    out_hbm,
    w, u, ub, rhs, factor, diag, res,
    lat_out, lat_in, dn_out, dn_in, h_out, h_in,
    load_sem, w_sem, out_sem,
    lat_send, lat_recv, dn_send, dn_recv, h_send, h_recv,
):
    side = math.isqrt(nodes)
    far = max(2, lat_count // 8)
    offsets = (-1, 1, -far, far)
    p = lax.axis_index("lat")
    r = lax.axis_index("rad")
    size = nodes // CHUNKS
    lanes = u.shape[1]
    upper, lower = slice(0, 4 * nodes), slice(4 * nodes, 6 * nodes)

    load_u = pltpu.make_async_copy(start_hbm.at[0, 0], u, load_sem.at[0])
    load_rhs = pltpu.make_async_copy(source_hbm.at[0, 0], rhs, load_sem.at[1])
    load_factor = pltpu.make_async_copy(decay_hbm.at[0, 0], factor, load_sem.at[2])
    load_w = [
        pltpu.make_async_copy(w_hbm.at[0, 0, part], w.at[part], w_sem.at[n])
        for n, part in enumerate((upper, lower))
    ]
    load_u.start()
    for copy in load_w:
        copy.start()
    load_rhs.start()
    load_factor.start()

    barrier = pltpu.get_barrier_semaphore()
    for offset in offsets:
        target = (p - offset + lat_count) % lat_count
        pl.semaphore_signal(barrier, inc=1, device_id={"lat": target}, device_id_type=MESH)

    below, above = (r - 1 + rad_count) % rad_count, (r + 1) % rad_count

    @pl.when(r > 0)
    def _():
        pl.semaphore_signal(barrier, inc=1, device_id={"rad": below}, device_id_type=MESH)

    @pl.when(r < rad_count - 1)
    def _():
        pl.semaphore_signal(barrier, inc=1, device_id={"rad": above}, device_id_type=MESH)

    inner = (r + rad_count - 1) // rad_count + (2 * rad_count - 2 - r) // rad_count
    pl.semaphore_wait(barrier, len(offsets) + inner)

    def lat_copy(outer, k):
        target = (p - offsets[k] + lat_count) % lat_count
        return pltpu.make_async_remote_copy(
            src_ref=lat_out.at[outer, k], dst_ref=lat_in.at[outer, k],
            send_sem=lat_send.at[outer, k], recv_sem=lat_recv.at[outer, k],
            device_id={"lat": target}, device_id_type=MESH,
        )

    def dn_copy(sweep):
        return pltpu.make_async_remote_copy(
            src_ref=dn_out.at[sweep], dst_ref=dn_in.at[sweep],
            send_sem=dn_send.at[sweep], recv_sem=dn_recv.at[sweep],
            device_id={"rad": below}, device_id_type=MESH,
        )

    def h_copy(sweep, c):
        rows = pl.ds(c * size, size)
        return pltpu.make_async_remote_copy(
            src_ref=h_out.at[sweep, rows], dst_ref=h_in.at[sweep, rows],
            send_sem=h_send.at[sweep, c], recv_sem=h_recv.at[sweep, c],
            device_id={"rad": above}, device_id_type=MESH,
        )

    def send_faces(outer):
        for k in SEND_ORDER:
            target = (p - offsets[k] + lat_count) % lat_count
            which = jnp.full((nodes, lanes), face_at[k, target], jnp.int32)
            face = u[slice(0, nodes), :]
            for f in range(1, 4):
                face = jnp.where(which == f, u[slice(f * nodes, (f + 1) * nodes), :], face)
            lat_out[outer, k] = permuted(face, code_at[k, target], side)
            lat_copy(outer, k).start()

    def residual(part):
        applied = jnp.dot(w[part, :], ub[...], preferred_element_type=jnp.float32)
        return rhs[part, :] - (applied + diag[part, :] * u[part, :])

    load_u.wait()
    send_faces(0)
    ub[...] = u[...].astype(jnp.bfloat16)
    for block in range(6 * nodes // lanes):
        own = slice(block * lanes, (block + 1) * lanes)
        diag[own, :] = jnp.broadcast_to(diag_ref[0, :, own], (lanes, lanes)).T
    load_rhs.wait()
    load_factor.wait()
    for copy in load_w:
        copy.wait()

    for outer in range(ITERS):
        for part in (upper, lower):
            res[part, :] = residual(part)
        u[lower, :] = u[lower, :] + OMEGA * res[lower, :]
        ub[lower, :] = u[lower, :].astype(jnp.bfloat16)
        for k in SEND_ORDER:
            own = slice(k * nodes, (k + 1) * nodes)
            lat_copy(outer, k).wait_recv()
            new = u[own, :] + OMEGA * (res[own, :] + COUPLE * lat_in[outer, k])
            u[own, :] = new
            ub[own, :] = new.astype(jnp.bfloat16)
        for turn in range(RADIAL_PASSES):
            sweep = outer * RADIAL_PASSES + turn
            bottom = slice(4 * nodes, 5 * nodes)
            top = slice(5 * nodes, 6 * nodes)
            res[lower, :] = residual(lower)

            @pl.when(r > 0)
            def _():
                dn_out[sweep] = res[bottom, :]
                dn_copy(sweep).start()

            @pl.when(r == 0)
            def _():
                h_out[sweep] = factor[...] * res[top, :]
                for c in range(CHUNKS):
                    h_copy(sweep, c).start()

            new = u[upper, :] + OMEGA * residual(upper)
            u[upper, :] = new
            ub[upper, :] = new.astype(jnp.bfloat16)
            if turn == RADIAL_PASSES - 1:
                if outer < ITERS - 1:
                    send_faces(outer + 1)
                else:
                    pltpu.make_async_copy(
                        u.at[upper], out_hbm.at[0, 0, upper], out_sem.at[0]
                    ).start()

            @pl.when(r > 0)
            def _():
                for c in range(CHUNKS):
                    rows = slice(c * size, (c + 1) * size)
                    from_bottom = slice(4 * nodes + c * size, 4 * nodes + (c + 1) * size)
                    from_top = slice(5 * nodes + c * size, 5 * nodes + (c + 1) * size)
                    h_copy(sweep, c).wait_recv()

                    @pl.when(r < rad_count - 1)
                    def _():
                        h_out[sweep, rows] = factor[rows, :] * (h_in[sweep, rows] + res[from_top, :])
                        h_copy(sweep, c).start()

                    u[from_bottom, :] = u[from_bottom, :] + OMEGA * (
                        res[from_bottom, :] + COUPLE * h_in[sweep, rows]
                    )

            @pl.when(r == 0)
            def _():
                u[bottom, :] = u[bottom, :] + OMEGA * res[bottom, :]

            @pl.when(r < rad_count - 1)
            def _():
                dn_copy(sweep).wait_recv()
                u[top, :] = u[top, :] + OMEGA * (res[top, :] + COUPLE * dn_in[sweep])

            @pl.when(r == rad_count - 1)
            def _():
                u[top, :] = u[top, :] + OMEGA * res[top, :]

            ub[lower, :] = u[lower, :].astype(jnp.bfloat16)

    out_copies = [
        pltpu.make_async_copy(u.at[part], out_hbm.at[0, 0, part], out_sem.at[n])
        for n, part in enumerate((upper, lower))
    ]
    out_copies[1].start()
    for outer in range(ITERS):
        for k in SEND_ORDER:
            lat_copy(outer, k).wait_send()

    @pl.when(r > 0)
    def _():
        for sweep in range(ITERS * RADIAL_PASSES):
            dn_copy(sweep).wait_send()

    @pl.when(r < rad_count - 1)
    def _():
        for sweep in range(ITERS * RADIAL_PASSES):
            for c in range(CHUNKS):
                h_copy(sweep, c).wait_send()

    for copy in out_copies:
        copy.wait()


def per_device(lat_count, rad_count, schur_off, schur_diag, source, start, decay, neighbour_face, orientation):
    order, columns = source.shape[2:]
    nodes = order // 6
    sweeps = ITERS * RADIAL_PASSES
    faces = lambda *lead: pltpu.VMEM((*lead, nodes, columns), jnp.float32)
    dma = lambda *shape: pltpu.SemaphoreType.DMA(shape)
    smem = pl.BlockSpec(memory_space=pltpu.SMEM)
    vmem = pl.BlockSpec(memory_space=pltpu.VMEM)
    hbm = pl.BlockSpec(memory_space=pl.ANY)
    return pl.pallas_call(
        functools.partial(kernel, lat_count, rad_count, nodes),
        out_shape=jax.ShapeDtypeStruct(source.shape, jnp.float32),
        in_specs=[smem, smem, vmem, hbm, hbm, hbm, hbm],
        out_specs=hbm,
        scratch_shapes=[
            pltpu.VMEM((order, order), jnp.bfloat16),
            pltpu.VMEM((order, columns), jnp.float32),
            pltpu.VMEM((order, columns), jnp.bfloat16),
            pltpu.VMEM((order, columns), jnp.float32),
            faces(),
            pltpu.VMEM((order, columns), jnp.float32),
            pltpu.VMEM((order, columns), jnp.float32),
            faces(ITERS, 4), faces(ITERS, 4), faces(sweeps), faces(sweeps), faces(sweeps), faces(sweeps),
            dma(3), dma(2), dma(2),
            dma(ITERS, 4), dma(ITERS, 4), dma(sweeps), dma(sweeps),
            dma(sweeps, CHUNKS), dma(sweeps, CHUNKS),
        ],
        compiler_params=pltpu.CompilerParams(
            collective_id=0, has_side_effects=True, vmem_limit_bytes=60 * 1024 * 1024
        ),
        name="shell",
    )(neighbour_face.T, orientation.T, schur_diag, schur_off, source, start, decay)


def solution(mesh):
    lat_count, rad_count = mesh.shape["lat"], mesh.shape["rad"]
    return jax.shard_map(
        functools.partial(per_device, lat_count, rad_count),
        mesh=mesh,
        in_specs=(
            P("lat", "rad", None, None),
            P("lat", "rad", None),
            P("lat", "rad", None, None),
            P("lat", "rad", None, None),
            P("lat", "rad", None, None),
            P(),
            P(),
        ),
        out_specs=P("lat", "rad", None, None),
        check_vma=False,
    )
```

time: 177 us -> 52.2 us (0.29)
  the two profiles are of different devices: /device:TPU:0 before, /device:TPU:24 now
where the time goes in v1:
time: 52.2 us; the launch traced here: 52 us
  Pallas kernels  49.9 us (96%)
  local copies, waits for them, and re-layouts  2.06 us (4%)
    pallas_call x1, Pallas kernels, per_device(): pl.pallas_call(functools.partial(kernel, lat_count, rad_count, nodes), ou...  49.9 us
    unnamed x1, local copies, waits for them, and re-layouts  2.06 us

profile of v1, /device:TPU:24, one launch (start us, length us, event | category | flops | bytes accessed | tf_op | source)
XLA Modules:
  0.0 52.0 jit_solution(11526971404515203992)
XLA Ops:
  0.0 49.9 %shell.1 = f32[1,1,1536,128]{3,2,1,0:T(8,128)} custom-call(s32[4,8]{1,0:T(4,128)} %bitcast.2, s32[4,8]{1,0:T(4,128)} %bitcast.3, f32[1,1,1536]{2,1,0:T(1,128)} %diag_ref.1, bf16[1,1,1536,1536]{3,2,1,0:T(8,128)(2,1)} %w_hbm.1, f32[1,1,1536,128]{3,2,1,0:T(8,128)} %source_hbm.1, f32[1,1,1536,128]{3,2,1,0:T(8,128)} %start_hbm.1, f32[1,1,256,128]{3,2,1,0:T(8,128)} %decay_hbm.1), custom_call_target="tpu_custom_call" | custom-call | tf_op jit(solution)/shard_map/shell/pallas_call | solution.py:243
  49.9 2.1 %copy.9 = f32[1,1,1536,128]{3,2,1,0:T(8,128)} copy(f32[1,1,1536,128]{3,2,1,0:T(8,128)} %shell.1) | data formatting | bytes 1572864

commit v2 on v1

--- a/solution.py
+++ b/solution.py
@@ -12,7 +12,7 @@
 RADIAL_PASSES = 2
 OMEGA = 0.3
 COUPLE = 0.5
-CHUNKS = 4
+CHUNKS = 8
 SEND_ORDER = (2, 3, 0, 1)
 MESH = pl.DeviceIdType.MESH
 
@@ -42,10 +42,10 @@
 def kernel(
     lat_count, rad_count, nodes,
     face_at, code_at, diag_ref, w_hbm, source_hbm, start_hbm, decay_hbm,
-    out_hbm,
-    w, u, ub, rhs, factor, diag, res,
+    out_ref,
+    w, ub, rhs, factor, diag, res, ready,
     lat_out, lat_in, dn_out, dn_in, h_out, h_in,
-    load_sem, w_sem, out_sem,
+    load_sem, w_sem,
     lat_send, lat_recv, dn_send, dn_recv, h_send, h_recv,
 ):
     side = math.isqrt(nodes)
@@ -54,6 +54,7 @@
     p = lax.axis_index("lat")
     r = lax.axis_index("rad")
     size = nodes // CHUNKS
+    u = out_ref.at[0, 0]
     lanes = u.shape[1]
     upper, lower = slice(0, 4 * nodes), slice(4 * nodes, 6 * nodes)
 
@@ -86,7 +87,6 @@
         pl.semaphore_signal(barrier, inc=1, device_id={"rad": above}, device_id_type=MESH)
 
     inner = (r + rad_count - 1) // rad_count + (2 * rad_count - 2 - r) // rad_count
-    pl.semaphore_wait(barrier, len(offsets) + inner)
 
     def lat_copy(outer, k):
         target = (p - offsets[k] + lat_count) % lat_count
@@ -111,14 +111,17 @@
             device_id={"rad": above}, device_id_type=MESH,
         )
 
-    def send_faces(outer):
-        for k in SEND_ORDER:
+    def make_faces(outer, which_faces):
+        for k in which_faces:
             target = (p - offsets[k] + lat_count) % lat_count
             which = jnp.full((nodes, lanes), face_at[k, target], jnp.int32)
             face = u[slice(0, nodes), :]
             for f in range(1, 4):
                 face = jnp.where(which == f, u[slice(f * nodes, (f + 1) * nodes), :], face)
             lat_out[outer, k] = permuted(face, code_at[k, target], side)
+
+    def start_faces(outer, which_faces):
+        for k in which_faces:
             lat_copy(outer, k).start()
 
     def residual(part):
@@ -126,7 +129,12 @@
         return rhs[part, :] - (applied + diag[part, :] * u[part, :])
 
     load_u.wait()
-    send_faces(0)
+    make_faces(0, SEND_ORDER[:2])
+    pl.semaphore_wait(barrier, len(offsets) + inner)
+    start_faces(0, SEND_ORDER[:2])
+    for k in SEND_ORDER[2:]:
+        make_faces(0, (k,))
+        start_faces(0, (k,))
     ub[...] = u[...].astype(jnp.bfloat16)
     for block in range(6 * nodes // lanes):
         own = slice(block * lanes, (block + 1) * lanes)
@@ -141,17 +149,26 @@
             res[part, :] = residual(part)
         u[lower, :] = u[lower, :] + OMEGA * res[lower, :]
         ub[lower, :] = u[lower, :].astype(jnp.bfloat16)
+        ready[...] = jnp.dot(w[lower, lower], ub[lower, :], preferred_element_type=jnp.float32)
         for k in SEND_ORDER:
             own = slice(k * nodes, (k + 1) * nodes)
             lat_copy(outer, k).wait_recv()
             new = u[own, :] + OMEGA * (res[own, :] + COUPLE * lat_in[outer, k])
             u[own, :] = new
             ub[own, :] = new.astype(jnp.bfloat16)
+            if k != SEND_ORDER[-1]:
+                ready[...] = ready[...] + jnp.dot(
+                    w[lower, own], ub[own, :], preferred_element_type=jnp.float32
+                )
         for turn in range(RADIAL_PASSES):
             sweep = outer * RADIAL_PASSES + turn
             bottom = slice(4 * nodes, 5 * nodes)
             top = slice(5 * nodes, 6 * nodes)
-            res[lower, :] = residual(lower)
+            last = slice(SEND_ORDER[-1] * nodes, (SEND_ORDER[-1] + 1) * nodes) if turn == 0 else lower
+            applied = ready[...] + jnp.dot(
+                w[lower, last], ub[last, :], preferred_element_type=jnp.float32
+            )
+            res[lower, :] = rhs[lower, :] - (applied + diag[lower, :] * u[lower, :])
 
             @pl.when(r > 0)
             def _():
@@ -169,11 +186,11 @@
             ub[upper, :] = new.astype(jnp.bfloat16)
             if turn == RADIAL_PASSES - 1:
                 if outer < ITERS - 1:
-                    send_faces(outer + 1)
-                else:
-                    pltpu.make_async_copy(
-                        u.at[upper], out_hbm.at[0, 0, upper], out_sem.at[0]
-                    ).start()
+                    for k in SEND_ORDER:
+                        make_faces(outer + 1, (k,))
+                        start_faces(outer + 1, (k,))
+            else:
+                ready[...] = jnp.dot(w[lower, upper], ub[upper, :], preferred_element_type=jnp.float32)
 
             @pl.when(r > 0)
             def _():
@@ -207,11 +224,6 @@
 
             ub[lower, :] = u[lower, :].astype(jnp.bfloat16)
 
-    out_copies = [
-        pltpu.make_async_copy(u.at[part], out_hbm.at[0, 0, part], out_sem.at[n])
-        for n, part in enumerate((upper, lower))
-    ]
-    out_copies[1].start()
     for outer in range(ITERS):
         for k in SEND_ORDER:
             lat_copy(outer, k).wait_send()
@@ -226,9 +238,6 @@
         for sweep in range(ITERS * RADIAL_PASSES):
             for c in range(CHUNKS):
                 h_copy(sweep, c).wait_send()
-
-    for copy in out_copies:
-        copy.wait()
 
 
 def per_device(lat_count, rad_count, schur_off, schur_diag, source, start, decay, neighbour_face, orientation):
@@ -244,22 +253,22 @@
         functools.partial(kernel, lat_count, rad_count, nodes),
         out_shape=jax.ShapeDtypeStruct(source.shape, jnp.float32),
         in_specs=[smem, smem, vmem, hbm, hbm, hbm, hbm],
-        out_specs=hbm,
+        out_specs=vmem,
         scratch_shapes=[
             pltpu.VMEM((order, order), jnp.bfloat16),
-            pltpu.VMEM((order, columns), jnp.float32),
             pltpu.VMEM((order, columns), jnp.bfloat16),
             pltpu.VMEM((order, columns), jnp.float32),
             faces(),
             pltpu.VMEM((order, columns), jnp.float32),
             pltpu.VMEM((order, columns), jnp.float32),
+            pltpu.VMEM((2 * nodes, columns), jnp.float32),
             faces(ITERS, 4), faces(ITERS, 4), faces(sweeps), faces(sweeps), faces(sweeps), faces(sweeps),
-            dma(3), dma(2), dma(2),
+            dma(3), dma(2),
             dma(ITERS, 4), dma(ITERS, 4), dma(sweeps), dma(sweeps),
             dma(sweeps, CHUNKS), dma(sweeps, CHUNKS),
         ],
         compiler_params=pltpu.CompilerParams(
-            collective_id=0, has_side_effects=True, vmem_limit_bytes=60 * 1024 * 1024
+            collective_id=0, has_side_effects=True, vmem_limit_bytes=63 * 1024 * 1024
         ),
         name="shell",
     )(neighbour_face.T, orientation.T, schur_diag, schur_off, source, start, decay)

time: 52.2 us -> 50.2 us (0.962)
  Pallas kernels: 49.9 us -> 47.9 us
    pallas_call x1, Pallas kernels: 49.9 us -> 47.9 us  [per_device(): pl.pallas_call(functools.partial(kernel, lat_count, rad_count, nodes), ou...]
where the time goes in v2:
time: 50.2 us; the launch traced here: 50 us
  Pallas kernels  47.9 us (95%)
  local copies, waits for them, and re-layouts  2.06 us (4%)
    pallas_call x1, Pallas kernels, per_device(): pl.pallas_call(functools.partial(kernel, lat_count, rad_count, nodes), ou...  47.9 us
    unnamed x1, local copies, waits for them, and re-layouts  2.06 us

profile of v2, /device:TPU:24, one launch (start us, length us, event | category | flops | bytes accessed | tf_op | source)
XLA Modules:
  0.0 50.0 jit_solution(14798487892841765213)
XLA Ops:
  0.0 47.9 %shell.1 = f32[1,1,1536,128]{3,2,1,0:T(8,128)} custom-call(s32[4,8]{1,0:T(4,128)} %bitcast.2, s32[4,8]{1,0:T(4,128)} %bitcast.3, f32[1,1,1536]{2,1,0:T(1,128)} %diag_ref.1, bf16[1,1,1536,1536]{3,2,1,0:T(8,128)(2,1)} %w_hbm.1, f32[1,1,1536,128]{3,2,1,0:T(8,128)} %source_hbm.1, f32[1,1,1536,128]{3,2,1,0:T(8,128)} %start_hbm.1, f32[1,1,256,128]{3,2,1,0:T(8,128)} %decay_hbm.1), custom_call_target="tpu_custom_call" | custom-call | tf_op jit(solution)/shard_map/shell/pallas_call | solution.py:252
  47.9 2.1 %copy.9 = f32[1,1,1536,128]{3,2,1,0:T(8,128)} copy(f32[1,1,1536,128]{3,2,1,0:T(8,128)} %shell.1) | data formatting | bytes 1572864
